TPU v7x, 32 devices: a whole 2x2x4 slice. The times are simulated.
32 devices in a mesh: sample: 2 (over x), sy: 4 (over y, core), sz: 4 (over z).
Axes of the slice: x: 2, y: 2, z: 4, core: 2. Of those that a mesh axis runs over, the one named last changes fastest.
Arguments:
- volume: bfloat16 [2, 32, 16, 32, 128], P('sample', None, 'sz', 'sy'), may hold values from -22.5 to 22.5
- amax_history: float32 [4, 16], replicated, may hold values from 0.48 to 2.5
- conv_first: bfloat16 [27, 32, 32], replicated, may hold values from -0.21875 to 0.21875
- conv_second: bfloat16 [27, 32, 32], replicated, may hold values from -0.21875 to 0.21875
- conv_third: bfloat16 [27, 64, 32], P(None, 'sy'), may hold values from -0.21875 to 0.21875
- conv_fourth: bfloat16 [27, 64, 64], P(None, 'sy'), may hold values from -0.15625 to 0.15625
- gain_fine: float32 [2, 32], replicated, may hold values from 0.5 to 1.5
- shift_fine: float32 [2, 32], replicated, may hold values from -0.5 to 0.5
- gain_coarse: float32 [2, 64], P(None, 'sy'), may hold values from 0.5 to 1.5
- shift_coarse: float32 [2, 64], P(None, 'sy'), may hold values from -0.5 to 0.5
Outputs:
- skip_features: bfloat16 [2, 32, 16, 32, 128], P('sample', None, 'sz', 'sy')
- coarse_features: bfloat16 [2, 64, 8, 1024], P('sample', 'sy', 'sz')
- amax_now: float32 [4], replicated
All inputs are finite; a program needn't handle non-finite values.
Results may differ from a plain program's by a relative error of at most 0.012.
Values may be sent and summed in bfloat16 or wider, within the bound.
A program may use at most 128 MiB of HBM per device.

v0:
```python
import jax
import jax.numpy as jnp
from jax import lax
from jax.sharding import PartitionSpec as P

norm_eps = 1e-05
leak_slope = 0.01


def padded_2(cells, sides, width):
    for axis, dim in sides:
        count = lax.axis_size(axis)
        ends = count - 1
        head = lax.slice_in_dim(cells, 0, width, axis=dim)
        tail = lax.slice_in_dim(cells, cells.shape[dim] - width, cells.shape[dim], axis=dim)
        cells = jnp.concatenate(
            [
                lax.ppermute(tail, axis, [(i, (i + 1) % count) for i in range(ends)]),
                cells,
                lax.ppermute(head, axis, [((i + 1) % count, i) for i in range(ends)]),
            ],
            axis=dim,
        )
    return cells


def limited(values, bound):
    return jnp.clip(values.astype(jnp.float32), -bound, bound).astype(jnp.bfloat16)


def fine_faces(values):
    return padded_2(values, (("sy", 2), ("sz", 1)), 1)


def coarse_faces(values):
    return padded_2(values, (("sz", 1),), 1)


def fine_stats(values):
    flat_rows = values.reshape(values.shape[0], -1)
    return lax.psum(
        (jnp.sum(flat_rows, axis=1), jnp.sum(flat_rows * flat_rows, axis=1)), ("sy", "sz")
    )


def coarse_stats(values):
    flat_rows = values.reshape(values.shape[0], -1)
    return lax.psum((jnp.sum(flat_rows, axis=1), jnp.sum(flat_rows * flat_rows, axis=1)), "sz")


def apply_norm(values, moments, cell_count, gains, offset):
    chan_mean = moments[0] / cell_count
    spread = moments[1] / cell_count - chan_mean * chan_mean
    scaling = lax.rsqrt(spread + norm_eps) * gains
    shaped = (-1,) + (1,) * (values.ndim - 1)
    normed = (values - chan_mean.reshape(shaped)) * scaling.reshape(shaped) + offset.reshape(shaped)
    return jnp.where(normed >= 0, normed, leak_slope * normed).astype(jnp.bfloat16)


def level_one_conv(padded, weight):
    channels, depth_cells, height_cells, width_cells = padded.shape
    out_depth = depth_cells - 2
    out_height = height_cells - 2
    out_chan = weight.shape[1]
    widened = jnp.pad(padded, ((0, 0), (0, 0), (0, 0), (1, 1)))
    stacked = jnp.concatenate(
        [widened[:, :, :, x_tap : x_tap + width_cells] for x_tap in range(3)], axis=0
    )
    summed = jnp.zeros((out_chan, out_depth * out_height * width_cells), jnp.float32)
    for z_tap in range(3):
        for y_tap in range(3):
            first_tap = z_tap * 9 + y_tap * 3
            taps = weight[first_tap : first_tap + 3]
            matrix = jnp.transpose(taps, (1, 0, 2)).reshape(out_chan, 3 * channels)
            window = stacked[:, z_tap : z_tap + out_depth, y_tap : y_tap + out_height, :].reshape(
                3 * channels, -1
            )
            summed = summed + jnp.dot(matrix, window, preferred_element_type=jnp.float32)
    return summed.reshape(out_chan, out_depth, out_height, width_cells)


def level_two_conv(padded, weight, row_len):
    channels, depth_cells, flat_len = padded.shape
    out_depth = depth_cells - 2
    out_chan = weight.shape[1]
    column = lax.broadcasted_iota(jnp.int32, (1, 1, flat_len), 2) % row_len
    blank = jnp.zeros((), padded.dtype)
    sources = (
        jnp.where(column == row_len - 1, blank, padded),
        padded,
        jnp.where(column == 0, blank, padded),
    )
    wide_len = flat_len + 2 * row_len
    stacked = jnp.concatenate(
        [
            jnp.pad(sources[x_tap], ((0, 0), (0, 0), (row_len + 1, row_len + 1)))[
                :, :, x_tap : x_tap + wide_len
            ]
            for x_tap in range(3)
        ],
        axis=0,
    )
    summed = jnp.zeros((out_chan, out_depth * flat_len), jnp.float32)
    for z_tap in range(3):
        for y_tap in range(3):
            first_tap = z_tap * 9 + y_tap * 3
            taps = weight[first_tap : first_tap + 3]
            matrix = jnp.transpose(taps, (1, 0, 2)).reshape(out_chan, 3 * channels)
            window = stacked[
                :, z_tap : z_tap + out_depth, y_tap * row_len : y_tap * row_len + flat_len
            ].reshape(3 * channels, -1)
            summed = summed + jnp.dot(matrix, window, preferred_element_type=jnp.float32)
    return summed.reshape(out_chan, out_depth, flat_len)


def magnitude(values):
    return jnp.max(jnp.abs(values.astype(jnp.float32)))


def per_device(
    volume,
    amax_history,
    conv_first,
    conv_second,
    conv_third,
    conv_fourth,
    gain_fine,
    shift_fine,
    gain_coarse,
    shift_coarse,
):
    bounds = jnp.max(amax_history, axis=1)
    sample_count, channels, z_cells, y_cells, x_cells = volume.shape
    z_groups = lax.axis_size("sz")
    y_groups = lax.axis_size("sy")
    half_x = x_cells // 2
    half_z = z_cells // 2
    fine_cells = float(z_cells * z_groups * y_cells * y_groups * x_cells)
    coarse_cells = float(half_z * z_groups * (y_cells // 2) * y_groups * half_x)
    source = volume[0]
    layer_peaks = [magnitude(source)]
    first_in = limited(source, bounds[0])
    first_out = level_one_conv(fine_faces(first_in), conv_first)
    hidden = apply_norm(first_out, fine_stats(first_out), fine_cells, gain_fine[0], shift_fine[0])
    layer_peaks.append(magnitude(hidden))
    second_out = level_one_conv(fine_faces(limited(hidden, bounds[1])), conv_second)
    skip_out = apply_norm(
        second_out, fine_stats(second_out), fine_cells, gain_fine[1], shift_fine[1]
    )
    skip_list = [skip_out]
    blocks = skip_out.reshape(channels, half_z, 2, y_cells // 2, 2, half_x, 2)
    pooled = jnp.max(blocks, axis=(2, 4, 6))
    layer_peaks.append(magnitude(pooled))
    gathered = lax.all_gather(limited(pooled, bounds[2]), "sy", axis=2, tiled=True)
    flat_in = gathered.reshape(channels, half_z, -1)
    third_out = level_two_conv(coarse_faces(flat_in), conv_third, half_x)
    coarse_hidden = apply_norm(
        third_out, coarse_stats(third_out), coarse_cells, gain_coarse[0], shift_coarse[0]
    )
    layer_peaks.append(magnitude(coarse_hidden))
    edged = coarse_faces(limited(coarse_hidden, bounds[3]))
    fourth_out = level_two_conv(
        lax.all_gather(edged, "sy", axis=0, tiled=True), conv_fourth, half_x
    )
    coarse_list = [
        apply_norm(
            fourth_out, coarse_stats(fourth_out), coarse_cells, gain_coarse[1], shift_coarse[1]
        )
    ]
    peak_rows = [jnp.stack(layer_peaks)]
    peaks = jnp.max(jnp.stack(peak_rows), axis=0)
    peaks = lax.pmax(peaks, ("sample", "sy", "sz"))
    return (jnp.stack(skip_list), jnp.stack(coarse_list), peaks)


def solution(mesh):
    return jax.shard_map(
        per_device,
        mesh=mesh,
        in_specs=(
            P("sample", None, "sz", "sy", None),
            P(),
            P(),
            P(),
            P(None, "sy", None),
            P(None, "sy", None),
            P(),
            P(),
            P(None, "sy"),
            P(None, "sy"),
        ),
        out_specs=(P("sample", None, "sz", "sy", None), P("sample", "sy", "sz", None), P()),
        check_vma=False,
    )
```

profile of v0, /device:TPU:0, one launch (start us, length us, event | category | flops | bytes accessed | tf_op | source)
XLA Modules:
  0.0 249.3 jit_solution(14499063451682183801)
XLA Ops:
  0.6 0.8 reduce_max.58
  2.7 1.7 fusion.64
  4.5 2.4 collective-permute-start
  6.9 1.3 collective-permute-start.1
  8.2 0.8 slice_bitcast_fusion.47
  8.9 0.8 slice_bitcast_fusion.45
  9.7 0.9 slice_bitcast_fusion.36
  10.5 0.9 slice_bitcast_fusion.27
  11.4 0.9 slice_bitcast_fusion.18
  12.3 0.9 slice_bitcast_fusion.9
  13.2 1.7 fusion.57
  16.6 4.3 %collective-permute-start.2 = (bf16[32,1,10,128]{3,2,1,0:T(8,128)(2,1)S(1)}, bf16[32,1,10,128]{3,2,1,0:T(8,128)(2,1)S(1)}, u32[]{:S(2)}, u32[]{:S(2)}) collective-permute-start(bf16[32,1,10,128]{3,2,1,0:T(8,128)(2,1)S(1)} %get-tuple-element.55), channel_id=1, source_target_pairs={{0,1},{1,2},{2,3},{4,5},{5,6},{6,7},{8,9},{9,10},{10,11},{12,13},{... | collective-permute-start | bytes 245768 | tf_op jit(solution)/shard_map/ppermute | solution.py:18
  20.9 1.3 collective-permute-start.3
  22.3 1.2 collective-permute-done.2
  23.4 4.6 %collective-permute-done.3 = bf16[32,1,10,128]{3,2,1,0:T(8,128)(2,1)S(1)} collective-permute-done((bf16[32,1,10,128]{3,2,1,0:T(8,128)(2,1)S(1)}, bf16[32,1,10,128]{3,2,1,0:T(8,128)(2,1)S(1)}, u32[]{:S(2)}, u32[]{:S(2)}) %collective-permute-start.3) | collective-permute-done | bytes 81952 | tf_op jit(solution)/shard_map/ppermute | solution.py:20
  28.0 1.8 fusion.11
  30.2 1.2 pad_maximum_fusion
  31.4 1.5 fusion.77
  37.0 31.8 %all-reduce.9 = (f32[32]{0:T(128)S(1)}, f32[32]{0:T(128)S(1)}) all-reduce(f32[32]{0:T(128)S(1)} %get-tuple-element.119, f32[32]{0:T(128)S(1)} %reduce_sum.72), channel_id=1, replica_groups=mesh['sample'=2,'sy'=4,'sz'=4] {'sy','sz'}, use_global_device_ids=true, to_apply=%region_4.5 | all-reduce | flops 64 | bytes 512 | tf_op jit(solution)/shard_map/psum | solution.py:41
  68.8 0.8 minimum_convert_fusion
  69.7 1.3 collective-permute-start.4
  71.0 1.3 collective-permute-start.5
  76.4 1.2 collective-permute-done.5
  77.8 2.6 %collective-permute-start.6 = (bf16[32,1,10,128]{3,2,1,0:T(8,128)(2,1)S(1)}, bf16[32,1,10,128]{3,2,1,0:T(8,128)(2,1)S(1)}, u32[]{:S(2)}, u32[]{:S(2)}) collective-permute-start(bf16[32,1,10,128]{3,2,1,0:T(8,128)(2,1)S(1)} %get-tuple-element.53), channel_id=1, source_target_pairs={{0,1},{1,2},{2,3},{4,5},{5,6},{6,7},{8,9},{9,10},{10,11},{12,13},{... | collective-permute-start | bytes 245768 | tf_op jit(solution)/shard_map/ppermute | solution.py:18
  80.4 1.5 collective-permute-start.7
  81.9 0.8 abs_reduce_fusion
  82.9 4.4 %collective-permute-done.7 = bf16[32,1,10,128]{3,2,1,0:T(8,128)(2,1)S(1)} collective-permute-done((bf16[32,1,10,128]{3,2,1,0:T(8,128)(2,1)S(1)}, bf16[32,1,10,128]{3,2,1,0:T(8,128)(2,1)S(1)}, u32[]{:S(2)}, u32[]{:S(2)}) %collective-permute-start.7) | collective-permute-done | bytes 81952 | tf_op jit(solution)/shard_map/ppermute | solution.py:20
  87.3 1.8 select_maximum_fusion
  89.5 1.2 pad_maximum_fusion.1
  90.7 1.5 fusion.76
  96.9 30.0 %all-reduce.8 = (f32[32]{0:T(128)S(1)}, f32[32]{0:T(128)S(1)}) all-reduce(f32[32]{0:T(128)S(1)} %get-tuple-element.121, f32[32]{0:T(128)S(1)} %reduce_sum.74), channel_id=1, replica_groups=mesh['sample'=2,'sy'=4,'sz'=4] {'sy','sz'}, use_global_device_ids=true, to_apply=%region_8.9 | all-reduce | flops 64 | bytes 512 | tf_op jit(solution)/shard_map/psum | solution.py:41
  126.9 2.9 %fusion.16 = bf16[32,2,4,64]{0,3,2,1:T(8,128)(2,1)S(1)} fusion(f32[32]{0:T(128)S(1)} %get-tuple-element.105, f32[32]{0:T(128)S(1)} %get-tuple-element.116, f32[32,2,2,4,2,64,2]{0,6,5,4,3,2,1:T(2,128)S(1)} %bitcast.322, f32[32]{0:T(128)S(1)} %get-tuple-element.115), kind=kLoop, calls=%fused_computation.59 | loop fusion | flops 1032192 | bytes 557440 | tf_op jit(solution)/shard_map/reduce_max | solution.py:152
  130.7 8.9 %all_gather.6 = bf16[32,2,16,64]{3,0,1,2:T(8,128)(2,1)S(1)} all-gather(bf16[32,2,4,64]{3,0,1,2:T(8,128)(2,1)S(1)} %copy.195), channel_id=1, replica_groups=mesh['sample'=2,'sy'=4,'sz'=4] {'sy'}, dimensions={2}, use_global_device_ids=true | all-gather | bytes 163840 | tf_op jit(solution)/shard_map/all_gather | solution.py:154
  140.0 1.3 collective-permute-start.9
  141.3 4.8 %collective-permute-start.8 = (bf16[32,1,1024]{2,0,1:T(8,128)(2,1)S(1)}, bf16[32,1,1024]{2,0,1:T(8,128)(2,1)S(1)}, u32[]{:S(2)}, u32[]{:S(2)}) collective-permute-start(bf16[32,1,1024]{2,0,1:T(8,128)(2,1)S(1)} %get-tuple-element.82), channel_id=1, source_target_pairs={{0,1},{1,2},{2,3},{4,5},{5,6},{6,7},{8,9},{9,10},{10,11},{12,13},{... | collective-permute-start | bytes 196616 | tf_op jit(solution)/shard_map/ppermute | solution.py:18
  146.7 1.2 collective-permute-done.8
  151.5 11.7 %all-reduce.11 = (f32[16]{0:T(128)S(1)}, f32[16]{0:T(128)S(1)}) all-reduce(f32[16]{0:T(128)S(1)} %get-tuple-element.123, f32[16]{0:T(128)S(1)} %reduce_sum.76), channel_id=1, replica_groups=mesh['sample'=2,'sy'=4,'sz'=4] {'sz'}, use_global_device_ids=true, to_apply=%region_13.14 | all-reduce | flops 32 | bytes 256 | tf_op jit(solution)/shard_map/psum | solution.py:48
  163.9 0.9 minimum_convert_fusion.1
  164.9 2.0 collective-permute-start.10
  166.9 1.3 collective-permute-start.11
  168.2 2.6 %pad_maximum_fusion.11 = f32[4]{0:T(128)S(1)} fusion(f32[1]{0:T(128)} %bitcast.57, f32[1]{0:T(128)} %bitcast.56, f32[1]{0:T(128)} %bitcast.55, f32[1]{0:T(128)} %bitcast.54), kind=kLoop, calls=%fused_computation.203 | loop fusion | flops 12 | bytes 32 | tf_op jit(solution)/shard_map/stack | solution.py:170
  170.9 0.9 fusion.59
  171.8 41.5 %pmax.7 = f32[4]{0:T(128)} all-reduce(f32[4]{0:T(128)S(1)} %pad_maximum_fusion.11), channel_id=1, replica_groups=mesh['sample'=2,'sy'=4,'sz'=4] {'sample','sy','sz'}, use_global_device_ids=true, to_apply=%region_22.23 | all-reduce | flops 4 | bytes 32 | tf_op jit(solution)/shard_map/pmax | solution.py:172
  213.5 8.1 %all_gather.7 = bf16[64,4,1024]{2,1,0:T(4,128)(2,1)S(1)} all-gather(bf16[16,4,1024]{2,1,0:T(4,128)(2,1)S(1)} %pad_maximum_fusion.10), channel_id=1, replica_groups=mesh['sample'=2,'sy'=4,'sz'=4] {'sy'}, dimensions={0}, use_global_device_ids=true | all-gather | bytes 655360 | tf_op jit(solution)/shard_map/all_gather | solution.py:163
  223.3 3.0 %pad_maximum_fusion.2 = bf16[192,4,1152]{2,1,0:T(4,128)(2,1)S(1)} fusion(bf16[64,4,1152]{2,1,0:T(4,128)(2,1)S(1)} %pad_slice_fusion, bf16[64,4,1152]{2,1,0:T(4,128)(2,1)S(1)} %pad_slice_fusion.1, bf16[64,4,1152]{2,1,0:T(4,128)(2,1)S(1)} %pad_slice_fusion.2), kind=kLoop, calls=%fused_computation.39 | loop fusion | flops 1769472 | bytes 3538944 | tf_op jit(solution)/shard_map/concatenate | solution.py:94
  226.3 8.0 %fusion.78 = (bf16[192,2,1024]{2,1,0:T(2,128)(2,1)S(1)}, bf16[192,2,1024]{2,1,0:T(2,128)(2,1)S(1)}, bf16[192,2,1024]{2,1,0:T(2,128)(2,1)S(1)}, bf16[192,2,1024]{...) fusion(bf16[192,4,1152]{2,1,0:T(4,128)(2,1)S(1)} %pad_maximum_f, ...), kind=kLoop, calls=%fused_computation.218 | loop fusion | bytes 14155776 | tf_op jit(solution)/shard_map/slice | solution.py:109
  238.6 9.9 %all-reduce.10 = (f32[16]{0:T(128)S(1)}, f32[16]{0:T(128)S(1)}) all-reduce(f32[16]{0:T(128)S(1)} %get-tuple-element.125, f32[16]{0:T(128)S(1)} %reduce_sum.78), channel_id=1, replica_groups=mesh['sample'=2,'sy'=4,'sz'=4] {'sz'}, use_global_device_ids=true, to_apply=%region_17.18 | all-reduce | flops 32 | bytes 256 | tf_op jit(solution)/shard_map/psum | solution.py:48
  248.5 0.9 fusion.70
  (181 shorter events, 26.5 us)
Async XLA Ops:
  4.5 12.0 %collective-permute-start = (bf16[32,4,1,128]{3,2,1,0:T(2,128)(2,1)S(1)}, bf16[32,4,1,128]{3,2,1,0:T(2,128)(2,1)S(1)}, u32[]{:S(2)}, u32[]{:S(2)}) collective-permute-start(bf16[32,4,1,128]{3,2,1,0:T(2,128)(2,1)S(1)} %get-tuple-element.61), channel_id=1, source_target_pairs={{0,4},{4,8},{8,12},{1,5},{5,9},{9,13},{2,6},{6,10},{10,14},{3,7},{... | collective-permute-start | bytes 98312 | tf_op jit(solution)/shard_map/ppermute | solution.py:18
  6.9 9.6 %collective-permute-start.1 = (bf16[32,4,1,128]{3,2,1,0:T(2,128)(2,1)S(1)}, bf16[32,4,1,128]{3,2,1,0:T(2,128)(2,1)S(1)}, u32[]{:S(2)}, u32[]{:S(2)}) collective-permute-start(bf16[32,4,1,128]{3,2,1,0:T(2,128)(2,1)S(1)} %get-tuple-element.62), channel_id=1, source_target_pairs={{4,0},{8,4},{12,8},{5,1},{9,5},{13,9},{6,2},{10,6},{14,10},{7,3},{... | collective-permute-start | bytes 98312 | tf_op jit(solution)/shard_map/ppermute | solution.py:20
  16.6 6.8 %collective-permute-start.2 = (bf16[32,1,10,128]{3,2,1,0:T(8,128)(2,1)S(1)}, bf16[32,1,10,128]{3,2,1,0:T(8,128)(2,1)S(1)}, u32[]{:S(2)}, u32[]{:S(2)}) collective-permute-start(bf16[32,1,10,128]{3,2,1,0:T(8,128)(2,1)S(1)} %get-tuple-element.55), channel_id=1, source_target_pairs={{0,1},{1,2},{2,3},{4,5},{5,6},{6,7},{8,9},{9,10},{10,11},{12,13},{... | collective-permute-start | bytes 245768 | tf_op jit(solution)/shard_map/ppermute | solution.py:18
  20.9 7.1 %collective-permute-start.3 = (bf16[32,1,10,128]{3,2,1,0:T(8,128)(2,1)S(1)}, bf16[32,1,10,128]{3,2,1,0:T(8,128)(2,1)S(1)}, u32[]{:S(2)}, u32[]{:S(2)}) collective-permute-start(bf16[32,1,10,128]{3,2,1,0:T(8,128)(2,1)S(1)} %get-tuple-element.56), channel_id=1, source_target_pairs={{1,0},{2,1},{3,2},{5,4},{6,5},{7,6},{9,8},{10,9},{11,10},{13,12},{... | collective-permute-start | bytes 245768 | tf_op jit(solution)/shard_map/ppermute | solution.py:20
  35.8 33.0 %copy-start = (f32[2,32]{1,0:T(2,128)S(1)}, f32[2,32]{1,0:T(2,128)}, u32[]{:S(2)}) copy-start(f32[2,32]{1,0:T(2,128)} %param.16) | copy-start | bytes 772
  69.7 6.7 %collective-permute-start.4 = (bf16[32,4,1,128]{3,2,1,0:T(2,128)(2,1)S(1)}, bf16[32,4,1,128]{3,2,1,0:T(2,128)(2,1)S(1)}, u32[]{:S(2)}, u32[]{:S(2)}) collective-permute-start(bf16[32,4,1,128]{3,2,1,0:T(2,128)(2,1)S(1)} %get-tuple-element.59), channel_id=1, source_target_pairs={{0,4},{4,8},{8,12},{1,5},{5,9},{9,13},{2,6},{6,10},{10,14},{3,7},{... | collective-permute-start | bytes 98312 | tf_op jit(solution)/shard_map/ppermute | solution.py:18
  71.0 6.7 %collective-permute-start.5 = (bf16[32,4,1,128]{3,2,1,0:T(2,128)(2,1)S(1)}, bf16[32,4,1,128]{3,2,1,0:T(2,128)(2,1)S(1)}, u32[]{:S(2)}, u32[]{:S(2)}) collective-permute-start(bf16[32,4,1,128]{3,2,1,0:T(2,128)(2,1)S(1)} %get-tuple-element.60), channel_id=1, source_target_pairs={{4,0},{8,4},{12,8},{5,1},{9,5},{13,9},{6,2},{10,6},{14,10},{7,3},{... | collective-permute-start | bytes 98312 | tf_op jit(solution)/shard_map/ppermute | solution.py:20
  77.8 5.1 %collective-permute-start.6 = (bf16[32,1,10,128]{3,2,1,0:T(8,128)(2,1)S(1)}, bf16[32,1,10,128]{3,2,1,0:T(8,128)(2,1)S(1)}, u32[]{:S(2)}, u32[]{:S(2)}) collective-permute-start(bf16[32,1,10,128]{3,2,1,0:T(8,128)(2,1)S(1)} %get-tuple-element.53), channel_id=1, source_target_pairs={{0,1},{1,2},{2,3},{4,5},{5,6},{6,7},{8,9},{9,10},{10,11},{12,13},{... | collective-permute-start | bytes 245768 | tf_op jit(solution)/shard_map/ppermute | solution.py:18
  80.4 6.9 %collective-permute-start.7 = (bf16[32,1,10,128]{3,2,1,0:T(8,128)(2,1)S(1)}, bf16[32,1,10,128]{3,2,1,0:T(8,128)(2,1)S(1)}, u32[]{:S(2)}, u32[]{:S(2)}) collective-permute-start(bf16[32,1,10,128]{3,2,1,0:T(8,128)(2,1)S(1)} %get-tuple-element.54), channel_id=1, source_target_pairs={{1,0},{2,1},{3,2},{5,4},{6,5},{7,6},{9,8},{10,9},{11,10},{13,12},{... | collective-permute-start | bytes 245768 | tf_op jit(solution)/shard_map/ppermute | solution.py:20
  140.0 8.0 %collective-permute-start.9 = (bf16[32,1,1024]{2,0,1:T(8,128)(2,1)S(1)}, bf16[32,1,1024]{2,0,1:T(8,128)(2,1)S(1)}, u32[]{:S(2)}, u32[]{:S(2)}) collective-permute-start(bf16[32,1,1024]{2,0,1:T(8,128)(2,1)S(1)} %get-tuple-element.81), channel_id=1, source_target_pairs={{1,0},{2,1},{3,2},{5,4},{6,5},{7,6},{9,8},{10,9},{11,10},{13,12},{... | collective-permute-start | bytes 196616 | tf_op jit(solution)/shard_map/ppermute | solution.py:20
  141.3 6.7 %collective-permute-start.8 = (bf16[32,1,1024]{2,0,1:T(8,128)(2,1)S(1)}, bf16[32,1,1024]{2,0,1:T(8,128)(2,1)S(1)}, u32[]{:S(2)}, u32[]{:S(2)}) collective-permute-start(bf16[32,1,1024]{2,0,1:T(8,128)(2,1)S(1)} %get-tuple-element.82), channel_id=1, source_target_pairs={{0,1},{1,2},{2,3},{4,5},{5,6},{6,7},{8,9},{9,10},{10,11},{12,13},{... | collective-permute-start | bytes 196616 | tf_op jit(solution)/shard_map/ppermute | solution.py:18
  149.9 13.3 %copy-start.1 = (f32[2,16]{1,0:T(2,128)S(1)}, f32[2,16]{1,0:T(2,128)}, u32[]{:S(2)}) copy-start(f32[2,16]{1,0:T(2,128)} %param.18) | copy-start | bytes 388
  164.9 48.3 %collective-permute-start.10 = (bf16[16,1,1024]{2,1,0:T(2,128)(2,1)S(1)}, bf16[16,1,1024]{2,1,0:T(2,128)(2,1)S(1)}, u32[]{:S(2)}, u32[]{:S(2)}) collective-permute-start(bf16[16,1,1024]{2,1,0:T(2,128)(2,1)S(1)} %get-tuple-element.101), channel_id=1, source_target_pairs={{0,1},{1,2},{2,3},{4,5},{5,6},{6,7},{8,9},{9,10},{10,11},{12,13},{... | collective-permute-start | bytes 98312 | tf_op jit(solution)/shard_map/ppermute | solution.py:18
  166.9 46.3 %collective-permute-start.11 = (bf16[16,1,1024]{2,1,0:T(2,128)(2,1)S(1)}, bf16[16,1,1024]{2,1,0:T(2,128)(2,1)S(1)}, u32[]{:S(2)}, u32[]{:S(2)}) collective-permute-start(bf16[16,1,1024]{2,1,0:T(2,128)(2,1)S(1)} %get-tuple-element.102), channel_id=1, source_target_pairs={{1,0},{2,1},{3,2},{5,4},{6,5},{7,6},{9,8},{10,9},{11,10},{13,12},{... | collective-permute-start | bytes 98312 | tf_op jit(solution)/shard_map/ppermute | solution.py:20
where the time goes:
time: 250 us; the launch traced here: 249 us
  blocking collectives  142 us (57%)
  local copies, waits for them, and re-layouts  27.2 us (11%)
  other arithmetic  26.6 us (11%)
  starting transfers between devices  25.3 us (10%)
  waiting for transfers between devices  12.9 us (5%)
  matrix products  11.3 us (5%)
  between operations  3.99 us (2%)
    psum x2, blocking collectives, fine_stats(): lax.psum((jnp.sum(flat_rows, axis=1), jnp.sum(flat_rows * flat_rows, axis...  61.8 us
    pmax x1, blocking collectives, per_device(): peaks = lax.pmax(peaks, ('sample', 'sy', 'sz'))  41.5 us
    psum x2, blocking collectives, coarse_stats(): lax.psum((jnp.sum(flat_rows, axis=1), jnp.sum(flat_rows * flat_rows, axis...  21.6 us
    ppermute x6, starting transfers between devices, padded_2(): lax.ppermute(tail, axis, [(i, (i + 1) % count) for i in range(ends)])  17.4 us
    ppermute x6, waiting for transfers between devices, padded_2(): lax.ppermute(head, axis, [((i + 1) % count, i) for i in range(ends)])  10.2 us
    all_gather x1, blocking collectives, per_device(): lax.all_gather(limited(pooled, bounds[2]), 'sy', axis=2, tiled=True)  8.94 us
    all_gather x1, blocking collectives, per_device(): lax.all_gather(edged, 'sy', axis=0, tiled=True)  8.15 us
    slice x1, local copies, waits for them, and re-layouts, level_two_conv(): stacked[:, z_tap:z_tap + out_depth, y_tap * row_len:y_tap * row_len + fla...  8.01 us
  transfers between devices with their start and end apart: 12, of which 6 were waited for; matrix products, arithmetic and copies ran while one was open for 6% of the time, Pallas kernels for 0%

commit v1 on v0

v1 whole, which is shorter than its diff:
```python
import functools

import jax
import jax.numpy as jnp
from jax import lax
from jax.experimental import pallas as pl
from jax.experimental.pallas import tpu as pltpu
from jax.sharding import PartitionSpec as P

norm_eps = 1e-05
leak_slope = 0.01
LANES = 128
MESH = pl.DeviceIdType.MESH
F32 = jnp.float32
BF16 = jnp.bfloat16
STEPS = ((-1, 0), (1, 0), (0, -1), (0, 1), (-1, -1), (-1, 1), (1, -1), (1, 1))


def iota(shape, dim):
    return lax.broadcasted_iota(jnp.int32, shape, dim)


def lane_row(column, start):
    n = column.shape[0]
    here = iota((n, LANES), 1) == iota((n, LANES), 0) + start
    return jnp.sum(jnp.where(here, column, 0.0), axis=0, keepdims=True)


def to_column(row, n, start):
    shape = (n, row.shape[1])
    here = iota(shape, 1) == iota(shape, 0) + start
    return jnp.sum(jnp.where(here, row, 0.0), axis=1, keepdims=True)


def leaky(normed):
    return jnp.where(normed >= 0, normed, leak_slope * normed).astype(BF16)


def remote(src, dst, send, recv, where):
    return pltpu.make_async_remote_copy(
        src_ref=src, dst_ref=dst, send_sem=send, recv_sem=recv, device_id=where, device_id_type=MESH
    )


def network(
    sizes,
    vol, hist, w1, w2, w3, w4, gf, sf, gc, sc,
    skip_out, coarse_out, peak_out,
    stacked, prod, vals, hid, zface, yface, corner,
    pool, wide3, g3, prod3, vals3, hid3, wide4, g4,
    stat, peak, peak_all,
    halo_s, halo_r, stat_s, stat_r, co_s, co_r, pk_s, pk_r, pa_s, pa_r,
):
    ns, ny, nz = sizes
    zc, yc, ch, xc = vol.shape
    hz, pairs = zc // 2, yc // 4
    tiles = pairs * ny
    oc = w3.shape[0] // 3
    group = ny * nz
    my_s, my_y, my_z = lax.axis_index("sample"), lax.axis_index("sy"), lax.axis_index("sz")
    me = my_y * nz + my_z

    def member(index):
        return {"sy": index // nz, "sz": lax.rem(index, nz)}

    barrier = pltpu.get_barrier_semaphore()
    for k in range(1, group):
        pl.semaphore_signal(barrier, inc=1, device_id=member(lax.rem(me + k, group)), device_id_type=MESH)
    for k in range(1, ns):
        pl.semaphore_signal(
            barrier, inc=1, device_id={"sample": lax.rem(my_s + k, ns)}, device_id_type=MESH
        )
    pl.semaphore_wait(barrier, group - 1 + ns - 1)

    lane = iota((ch, LANES), 1)
    bounds = [jnp.max(hist[l : l + 1, :]) for l in range(4)]

    def inside(dz, dy):
        z, y = my_z + dz, my_y + dy
        return (z >= 0) & (z < nz) & (y >= 0) & (y < ny)

    def halo(src, layer, d):
        dz, dy = STEPS[d]
        zi = 0 if dz < 0 else zc - 1
        yi = 0 if dy < 0 else yc - 1
        if dy == 0:
            src, dst = src.at[zi], zface.at[layer, int(dz < 0)]
        elif dz == 0:
            src, dst = src.at[:, yi], yface.at[layer, int(dy < 0)]
        else:
            src, dst = src.at[zi, yi], corner.at[layer, int(dz < 0) * 2 + int(dy < 0)]
        where = {"sy": jnp.clip(my_y + dy, 0, ny - 1), "sz": jnp.clip(my_z + dz, 0, nz - 1)}
        return remote(src, dst, halo_s.at[layer, d], halo_r.at[layer, d], where), dst

    def halo_start(src, layer):
        for d, (dz, dy) in enumerate(STEPS):
            @pl.when(inside(dz, dy))
            def _():
                halo(src, layer, d)[0].start()

            @pl.when(jnp.logical_not(inside(-dz, -dy)))
            def _():
                dst = halo(src, layer, d)[1]
                dst[...] = jnp.zeros(dst.shape, dst.dtype)

    def halo_wait(src, layer):
        for d, (dz, dy) in enumerate(STEPS):
            @pl.when(inside(-dz, -dy))
            def _():
                halo(src, layer, d)[0].wait_recv()

            @pl.when(inside(dz, dy))
            def _():
                halo(src, layer, d)[0].wait_send()

    def put(zp, yp, values, bound):
        v = jnp.clip(values.astype(F32), -bound, bound)
        left = jnp.where(lane == 0, 0.0, pltpu.roll(v, 1, 1))
        right = jnp.where(lane == LANES - 1, 0.0, pltpu.roll(v, LANES - 1, 1))
        stacked[zp, yp] = jnp.concatenate([left, v, right], axis=0).astype(BF16)

    def put_inner(src, bound):
        def plane(z, top):
            for y in range(yc):
                v = src[z, y]
                top = jnp.maximum(top, jnp.abs(v.astype(F32)))
                put(z + 1, y + 1, v, bound)
            return top

        return jnp.max(lax.fori_loop(0, zc, plane, jnp.zeros((ch, LANES), F32)))

    def put_halo(layer, bound):
        for side in range(2):
            for y in range(yc):
                put(side * (zc + 1), y + 1, zface[layer, side, y], bound)
            for z in range(zc):
                put(z + 1, side * (yc + 1), yface[layer, side, z], bound)
            for other in range(2):
                put(side * (zc + 1), other * (yc + 1), corner[layer, side * 2 + other], bound)

    def fine_conv(w):
        def plane(zp, carry):
            for y in range(0, yc, 2):
                rows = [stacked[zp, y + i : y + i + 3].reshape(9 * ch, LANES) for i in range(2)]
                prod[zp, y // 2] = jnp.dot(
                    w[...], jnp.concatenate(rows, axis=1), preferred_element_type=F32
                )
            return carry

        lax.fori_loop(0, zc + 2, plane, 0)

        def total(z, carry):
            s, q = carry
            for y in range(yc // 2):
                v = (
                    prod[z, y, 0:ch, :]
                    + prod[z + 1, y, ch : 2 * ch, :]
                    + prod[z + 2, y, 2 * ch : 3 * ch, :]
                )
                for i in range(2):
                    part = v[:, i * LANES : (i + 1) * LANES]
                    vals[z, 2 * y + i] = part
                    s, q = s + part, q + part * part
            return s, q

        zero = jnp.zeros((ch, LANES), F32)
        return lax.fori_loop(0, zc, total, (zero, zero))

    def share(buf, row, index, count, send, recv, where):
        buf[index] = jnp.broadcast_to(row, (8, LANES))

        def copy(k, slot):
            other = lax.rem(index + k, count)
            at = index if slot == "mine" else other
            return remote(buf.at[at], buf.at[at], send.at[k], recv.at[at], where(other))

        for k in range(1, count):
            copy(k, "mine").start()
        return copy

    def shared(copy, count):
        for k in range(1, count):
            copy(k, "theirs").wait_recv()
            copy(k, "mine").wait_send()

    def moments(phase, s, q, index, count, where, cells, gain_row, shift_row):
        n = s.shape[0]
        row = lane_row(jnp.sum(s, axis=1, keepdims=True), 0) + lane_row(
            jnp.sum(q, axis=1, keepdims=True), LANES // 2
        )
        buf = stat.at[phase]
        shared(share(buf, row, index, count, stat_s.at[phase], stat_r.at[phase], where), count)
        total = buf[0, 0:1, :]
        for i in range(1, count):
            total = total + buf[i, 0:1, :]
        mean = to_column(total, n, 0) / cells
        spread = to_column(total, n, LANES // 2) / cells - mean * mean
        scaling = lax.rsqrt(spread + norm_eps) * to_column(gain_row, n, 0)
        return mean, scaling, to_column(shift_row, n, 0)

    def fine_act(dst, phase, s, q):
        cells = float(zc * nz * yc * ny * xc)
        mean, scaling, offset = moments(
            phase, s, q, me, group, member, cells, gf[phase : phase + 1, :], sf[phase : phase + 1, :]
        )
        mean, scaling, offset = (jnp.broadcast_to(a, (ch, LANES)) for a in (mean, scaling, offset))

        def plane(z, carry):
            for y in range(yc):
                dst[z, y] = leaky((vals[z, y] - mean) * scaling + offset)
            return carry

        lax.fori_loop(0, zc, plane, 0)

    halo_start(vol, 0)
    peak0 = put_inner(vol, bounds[0])
    halo_wait(vol, 0)
    put_halo(0, bounds[0])
    s, q = fine_conv(w1)
    fine_act(hid, 0, s, q)
    halo_start(hid, 1)
    peak1 = put_inner(hid, bounds[1])
    halo_wait(hid, 1)
    put_halo(1, bounds[1])
    s, q = fine_conv(w2)
    fine_act(skip_out, 1, s, q)

    src_lane, dst_lane = iota((LANES, LANES), 0), iota((LANES, LANES), 1)
    half = LANES // 2
    pick = [
        jnp.where((dst_lane // half == i) & (src_lane == 2 * (dst_lane - i * half)), 1.0, 0.0).astype(BF16)
        for i in range(2)
    ]
    top = jnp.zeros((ch, LANES), F32)
    for z in range(hz):
        for t in range(pairs):
            found = jnp.zeros((ch, LANES), F32)
            for i in range(2):
                y = 4 * t + 2 * i
                block = [skip_out[2 * z + a, y + b].astype(F32) for a in range(2) for b in range(2)]
                m = jnp.maximum(jnp.maximum(block[0], block[1]), jnp.maximum(block[2], block[3]))
                m = jnp.maximum(m, pltpu.roll(m, LANES - 1, 1))
                found = found + jnp.dot(m.astype(BF16), pick[i], preferred_element_type=F32)
            top = jnp.maximum(top, jnp.abs(found))
            cells = jnp.clip(found, -bounds[2], bounds[2]).astype(BF16)
            pool[z, t] = cells
            g3[z + 1, my_y * pairs + t] = cells
    peak2 = jnp.max(top)

    def coarse_copies(layer, src, block_of, slab_of):
        out = []
        send, recv = co_s.at[layer], co_r.at[layer]
        for k in range(1, ny):
            other = lax.rem(my_y + k, ny)
            out.append((
                None,
                remote(src, slab_of(my_y), send.at[0, k], recv.at[0, my_y], {"sy": other}),
                None,
                remote(src, slab_of(other), send.at[0, k], recv.at[0, other], {"sy": other}),
            ))
        for kind, (step, plane, to) in enumerate(((-1, 0, hz + 1), (1, hz - 1, 0)), start=1):
            z = jnp.clip(my_z + step, 0, nz - 1)
            sends = (my_z + step >= 0) & (my_z + step < nz)
            gets = (my_z - step >= 0) & (my_z - step < nz)
            for y in range(ny):
                where = {"sy": y, "sz": z}
                out.append((
                    sends,
                    remote(src.at[plane], block_of(to, my_y), send.at[kind, y], recv.at[kind, my_y], where),
                    gets,
                    remote(src.at[plane], block_of(to, y), send.at[kind, y], recv.at[kind, y], where),
                ))
        return out

    def guarded(flag, act):
        if flag is None:
            act()
        else:
            pl.when(flag)(act)

    def coarse_start(copies, buf):
        for sends, mine, _, _ in copies:
            guarded(sends, mine.start)
        for at, missing in ((0, my_z == 0), (hz + 1, my_z == nz - 1)):
            @pl.when(missing)
            def _():
                buf[at] = jnp.zeros(buf.shape[1:], buf.dtype)

    def coarse_wait(copies):
        for sends, mine, gets, theirs in copies:
            guarded(gets, theirs.wait_recv)
            guarded(sends, mine.wait_send)

    def widen(load, n, wide):
        where = iota((n, LANES), 1)
        column = lax.rem(where, half)
        low = iota((3 * n, LANES), 1) < half

        def plane(z, carry):
            def put3(k, t, v):
                wide[z, k * 3 * n : (k + 1) * 3 * n, t * LANES : (t + 1) * LANES] = v.astype(BF16)

            before = jnp.zeros((3 * n, LANES), F32)
            for t in range(tiles):
                v = load(z, t).astype(F32)
                left = jnp.where(column == 0, 0.0, pltpu.roll(v, 1, 1))
                right = jnp.where(column == half - 1, 0.0, pltpu.roll(v, LANES - 1, 1))
                x = jnp.concatenate([left, v, right], axis=0)
                u = pltpu.roll(x, half, 1)
                put3(1, t, x)
                put3(0, t, jnp.where(low, before, u))
                if t:
                    put3(2, t - 1, jnp.where(low, before, u))
                before = u
            put3(2, tiles - 1, jnp.where(low, before, 0.0))
            return carry

        lax.fori_loop(0, hz + 2, plane, 0)

    def coarse_conv(w, wide):
        def plane(z, carry):
            prod3[z] = jnp.dot(w[...], wide[z], preferred_element_type=F32)
            return carry

        lax.fori_loop(0, hz + 2, plane, 0)
        s = q = jnp.zeros((oc, LANES), F32)
        for z in range(hz):
            for t in range(tiles):
                cols = slice(t * LANES, (t + 1) * LANES)
                v = (
                    prod3[z, 0:oc, cols]
                    + prod3[z + 1, oc : 2 * oc, cols]
                    + prod3[z + 2, 2 * oc : 3 * oc, cols]
                )
                vals3[z, :, cols] = v
                s, q = s + v, q + v * v
        return s, q

    coarse_cells = float(hz * nz * tiles * LANES)

    def slab(index):
        return {"sz": index}

    copies = coarse_copies(
        0,
        pool,
        lambda plane, y: g3.at[plane, pl.ds(y * pairs, pairs)],
        lambda y: g3.at[pl.ds(1, hz), pl.ds(y * pairs, pairs)],
    )
    coarse_start(copies, g3)
    coarse_wait(copies)
    widen(lambda z, t: g3[z, t], ch, wide3)
    s, q = coarse_conv(w3, wide3)
    mean, scaling, offset = moments(2, s, q, my_z, nz, slab, coarse_cells, gc[0:1, :], sc[0:1, :])
    top = jnp.zeros((oc, tiles * LANES), F32)
    for z in range(hz):
        v = leaky((vals3[z] - mean) * scaling + offset).astype(F32)
        top = jnp.maximum(top, jnp.abs(v))
        v = jnp.clip(v, -bounds[3], bounds[3]).astype(BF16)
        hid3[z] = v
        g4[z + 1, my_y] = v
    peak3 = jnp.max(top)
    copies = coarse_copies(
        1, hid3, lambda plane, y: g4.at[plane, y], lambda y: g4.at[pl.ds(1, hz), y]
    )
    coarse_start(copies, g4)

    at = iota((1, LANES), 1)
    row = jnp.zeros((1, LANES), F32)
    for i, value in enumerate((peak0, peak1, peak2, peak3)):
        row = jnp.where(at == i, value, row)
    peaks = share(peak, row, me, group, pk_s, pk_r, member)
    coarse_wait(copies)
    widen(
        lambda z, t: g4[z, :, :, t * LANES : (t + 1) * LANES].reshape(ny * oc, LANES), ny * oc, wide4
    )
    shared(peaks, group)
    row = peak[0, 0:1, :]
    for i in range(1, group):
        row = jnp.maximum(row, peak[i, 0:1, :])
    peaks = share(peak_all, row, my_s, ns, pa_s, pa_r, lambda index: {"sample": index})
    s, q = coarse_conv(w4, wide4)
    mean, scaling, offset = moments(3, s, q, my_z, nz, slab, coarse_cells, gc[1:2, :], sc[1:2, :])
    for z in range(hz):
        coarse_out[z] = leaky((vals3[z] - mean) * scaling + offset)
    shared(peaks, ns)
    row = peak_all[0]
    for i in range(1, ns):
        row = jnp.maximum(row, peak_all[i])
    peak_out[...] = row


def per_device(sizes, volume, hist, c1, c2, c3, c4, gf, sf, gc, sc):
    ns, ny, nz = sizes
    _, ch, zc, yc, xc = volume.shape
    oc = c3.shape[1]
    hz, pairs = zc // 2, yc // 4
    tiles = pairs * ny
    flat = tiles * LANES
    assert xc == LANES and zc % 2 == 0 and yc % 4 == 0

    def matrix(w):
        taps, out, inner = w.shape
        w = w.reshape(3, 9, out, inner)
        return jnp.transpose(w, (0, 2, 1, 3)).reshape(3 * out, 9 * inner)

    vmem = pl.BlockSpec(memory_space=pltpu.VMEM)
    dma = pltpu.SemaphoreType.DMA
    group = ny * nz
    skip, coarse, peaks = pl.pallas_call(
        functools.partial(network, sizes),
        out_shape=(
            jax.ShapeDtypeStruct((zc, yc, ch, xc), BF16),
            jax.ShapeDtypeStruct((hz, oc, flat), BF16),
            jax.ShapeDtypeStruct((8, LANES), F32),
        ),
        in_specs=[vmem] * 10,
        out_specs=(vmem,) * 3,
        scratch_shapes=[
            pltpu.VMEM((zc + 2, yc + 2, 3 * ch, LANES), BF16),
            pltpu.VMEM((zc + 2, yc // 2, 3 * ch, 2 * LANES), F32),
            pltpu.VMEM((zc, yc, ch, LANES), F32),
            pltpu.VMEM((zc, yc, ch, LANES), BF16),
            pltpu.VMEM((2, 2, yc, ch, LANES), BF16),
            pltpu.VMEM((2, 2, zc, ch, LANES), BF16),
            pltpu.VMEM((2, 4, ch, LANES), BF16),
            pltpu.VMEM((hz, pairs, ch, LANES), BF16),
            pltpu.VMEM((hz + 2, 9 * ch, flat), BF16),
            pltpu.VMEM((hz + 2, tiles, ch, LANES), BF16),
            pltpu.VMEM((hz + 2, 3 * oc, flat), F32),
            pltpu.VMEM((hz, oc, flat), F32),
            pltpu.VMEM((hz, oc, flat), BF16),
            pltpu.VMEM((hz + 2, 9 * oc * ny, flat), BF16),
            pltpu.VMEM((hz + 2, ny, oc, flat), BF16),
            pltpu.VMEM((4, group, 8, LANES), F32),
            pltpu.VMEM((group, 8, LANES), F32),
            pltpu.VMEM((ns, 8, LANES), F32),
            dma((2, 8)),
            dma((2, 8)),
            dma((4, group)),
            dma((4, group)),
            dma((2, 3, ny)),
            dma((2, 3, ny)),
            dma((group,)),
            dma((group,)),
            dma((ns,)),
            dma((ns,)),
        ],
        compiler_params=pltpu.CompilerParams(
            collective_id=0, has_side_effects=True, vmem_limit_bytes=56 * 1024 * 1024
        ),
    )(
        jnp.transpose(volume[0], (1, 2, 0, 3)),
        hist, matrix(c1), matrix(c2), matrix(c3), matrix(c4), gf, sf, gc, sc,
    )
    return (
        jnp.transpose(skip, (2, 0, 1, 3))[None],
        jnp.transpose(coarse, (1, 0, 2))[None],
        peaks[0, :4],
    )


def solution(mesh):
    sizes = (mesh.shape["sample"], mesh.shape["sy"], mesh.shape["sz"])
    return jax.shard_map(
        functools.partial(per_device, sizes),
        mesh=mesh,
        in_specs=(
            P("sample", None, "sz", "sy", None),
            P(),
            P(),
            P(),
            P(None, "sy", None),
            P(None, "sy", None),
            P(),
            P(),
            P(None, "sy"),
            P(None, "sy"),
        ),
        out_specs=(P("sample", None, "sz", "sy", None), P("sample", "sy", "sz", None), P()),
        check_vma=False,
    )
```

time: 250 us -> 62.8 us (0.25)
  blocking collectives: 142 us -> 0 us
  Pallas kernels: 0 us -> 52.1 us
  other arithmetic: 26.6 us -> 0 us
  starting transfers between devices: 25.3 us -> 0 us
  local copies, waits for them, and re-layouts: 27.2 us -> 9.61 us
  waiting for transfers between devices: 12.9 us -> 0 us
  matrix products: 11.3 us -> 0 us
  between operations: 3.99 us -> 0.71 us
    psum x4 -> x0, blocking collectives: 83.4 us -> none  [the longest x2 61.8 us: fine_stats(): lax.psum((jnp.sum(flat_rows, axis=1), jnp.sum(flat_rows * flat_rows, axis...]
    pallas_call x0 -> x1, Pallas kernels: none -> 52.1 us  [per_device(): pl.pallas_call(functools.partial(network, sizes), out_shape=(jax.ShapeDty...]
    pmax x1 -> x0, blocking collectives: 41.5 us -> none  [per_device(): peaks = lax.pmax(peaks, ('sample', 'sy', 'sz'))]
    ppermute x12 -> x0, starting transfers between devices: 25.3 us -> none  [the longest x6 17.4 us: padded_2(): lax.ppermute(tail, axis, [(i, (i + 1) % count) for i in range(ends)])]
    all_gather x2 -> x0, blocking collectives: 17.1 us -> none  [the longest x1 8.94 us: per_device(): lax.all_gather(limited(pooled, bounds[2]), 'sy', axis=2, tiled=True)]
    slice x15 -> x0, local copies, waits for them, and re-layouts: 14.3 us -> none  [the longest x1 8.01 us: level_two_conv(): stacked[:, z_tap:z_tap + out_depth, y_tap * row_len:y_tap * row_len + fla...]
    ppermute x12 -> x0, waiting for transfers between devices: 12.9 us -> none  [the longest x6 10.2 us: padded_2(): lax.ppermute(head, axis, [((i + 1) % count, i) for i in range(ends)])]
    dot_general x36 -> x0, matrix products: 11.3 us -> none  [the longest x18 7.54 us: level_one_conv(): jnp.dot(matrix, window, preferred_element_type=jnp.float32)]
  transfers between devices with their start and end apart: 12 -> 0, of which waited for: 6 -> 0; matrix products, arithmetic and copies ran while one was open for 6% -> 0% of each run, Pallas kernels for 0% -> 0%
where the time goes in v1:
time: 62.8 us; the launch traced here: 62.4 us
  Pallas kernels  52.1 us (83%)
  local copies, waits for them, and re-layouts  9.61 us (15%)
  between operations  0.71 us (1%)
    pallas_call x1, Pallas kernels, per_device(): pl.pallas_call(functools.partial(network, sizes), out_shape=(jax.ShapeDty...  52.1 us
    unnamed x13, local copies, waits for them, and re-layouts  3.69 us
    reshape x6, local copies, waits for them, and re-layouts, matrix(): return jnp.transpose(w, (0, 2, 1, 3)).reshape(3 * out, 9 * inner)  3.35 us
    reshape x4, local copies, waits for them, and re-layouts, matrix(): w = w.reshape(3, 9, out, inner)  1.39 us

profile of v1, /device:TPU:0, one launch (start us, length us, event | category | flops | bytes accessed | tf_op | source)
XLA Modules:
  0.0 62.4 jit_solution(12280478619993787668)
XLA Ops:
  0.6 0.9 %copy.34 = bf16[3,9,16,32]{3,1,2,0:T(8,128)(2,1)S(1)} copy(bf16[3,9,16,32]{3,2,1,0:T(8,128)(2,1)} %bitcast.37) | data formatting | bytes 55296 | tf_op jit(solution)/shard_map/reshape | solution.py:404
  1.6 0.0 copy-start.3
  1.6 0.7 %reshape.35.w3 = bf16[48,288]{1,0:T(8,128)(2,1)} reshape(bf16[3,16,9,32]{3,2,1,0:T(8,128)(2,1)S(1)} %bitcast.32) | data formatting | bytes 55296 | tf_op jit(solution)/shard_map/reshape | solution.py:405
  2.3 0.1 copy-done.3
  2.5 0.0 copy-start
  2.5 0.8 %reshape.37.w4 = bf16[48,576]{1,0:T(8,128)(2,1)} reshape(bf16[3,16,9,64]{3,2,1,0:T(8,128)(2,1)S(1)} %bitcast.33) | data formatting | bytes 110592 | tf_op jit(solution)/shard_map/reshape | solution.py:405
  3.3 0.1 copy-done
  3.4 0.0 copy-start.1
  3.4 0.8 %copy.32 = bf16[1,32,4,8,128]{4,1,3,2,0:T(8,128)(2,1)} copy(bf16[1,32,4,8,128]{4,3,2,1,0:T(8,128)(2,1)S(1)} %copy-done) | data formatting | bytes 524288 | tf_op args[0]
  4.2 0.1 copy-done.1
  4.4 0.2 copy.21
  4.6 0.0 copy-start.2
  4.6 0.2 reshape.31
  4.8 0.7 %copy.25.w1 = bf16[96,288]{1,0:T(8,128)(2,1)} copy(bf16[96,288]{0,1:T(8,128)(2,1)S(1)} %reshape.31) | data formatting | bytes 110592 | tf_op jit(solution)/shard_map/reshape | solution.py:405
  5.5 0.0 copy-done.2
  5.5 0.2 copy.22
  5.7 0.2 reshape.33
  5.9 0.7 %copy.26.w2 = bf16[96,288]{1,0:T(8,128)(2,1)} copy(bf16[96,288]{0,1:T(8,128)(2,1)S(1)} %reshape.33) | data formatting | bytes 110592 | tf_op jit(solution)/shard_map/reshape | solution.py:405
  6.6 52.1 %shard_map.121 = (bf16[4,8,32,128]{3,2,1,0:T(8,128)(2,1)}, bf16[2,16,1024]{2,1,0:T(8,128)(2,1)}, f32[8,128]{1,0:T(8,128)}) custom-call(bf16[4,8,32,128]{3,2,1,0:T(8,128)(2,1)} %bitcast.31, f32[4,16]{1,0:T(4,128)} %hist.1, bf16[96,288]{1,0:T(8,128)(2,1)} %copy.25.w1, bf16[96,288]{1,0:T(8,128)(2,1)} %copy.26.w2, bf16[48,288]{1,0:T(8,128)(2,1)} %reshape.35.w3, ...), custom_call_target="tpu_custom_call" | custom-call | tf_op jit(solution)/shard_map/pallas_call | solution.py:410
  58.7 0.0 copy-start.4
  58.8 1.8 %copy.27 = bf16[1,32,4,8,128]{4,3,2,1,0:T(8,128)(2,1)} copy(bf16[1,32,4,8,128]{4,1,3,2,0:T(8,128)(2,1)} %bitcast.34) | data formatting | bytes 524288
  60.5 0.0 copy-done.4
  60.5 0.7 %copy.28 = bf16[1,16,2,1024]{3,2,1,0:T(2,128)(2,1)} copy(bf16[1,16,2,1024]{3,1,2,0:T(8,128)(2,1)S(1)} %bitcast.39) | data formatting | bytes 131072
  61.2 1.2 %slice_bitcast_fusion = f32[4]{0:T(128)} fusion(f32[8,128]{1,0:T(8,128)} %get-tuple-element.8), kind=kLoop, calls=%fused_computation.3 | loop fusion | bytes 32 | tf_op jit(solution)/shard_map/squeeze | solution.py:459
  (1 shorter events, 0.0 us)
Async XLA Ops:
  1.6 0.9 %copy-start.3 = (bf16[27,16,64]{2,1,0:T(8,128)(2,1)S(1)}, bf16[27,16,64]{2,1,0:T(8,128)(2,1)}, u32[]{:S(2)}) copy-start(bf16[27,16,64]{2,1,0:T(8,128)(2,1)} %param.15) | copy-start | bytes 165892
  2.5 0.9 %copy-start = (bf16[1,32,4,8,128]{4,3,2,1,0:T(8,128)(2,1)S(1)}, bf16[1,32,4,8,128]{4,3,2,1,0:T(8,128)(2,1)}, u32[]{:S(2)}) copy-start(bf16[1,32,4,8,128]{4,3,2,1,0:T(8,128)(2,1)} %param.10) | copy-start | bytes 786436
  3.4 0.9 %copy-start.1 = (bf16[27,32,32]{2,1,0:T(8,128)(2,1)S(1)}, bf16[27,32,32]{2,1,0:T(8,128)(2,1)}, u32[]{:S(2)}) copy-start(bf16[27,32,32]{2,1,0:T(8,128)(2,1)} %param.12) | copy-start | bytes 165892
  4.6 0.9 %copy-start.2 = (bf16[27,32,32]{2,1,0:T(8,128)(2,1)S(1)}, bf16[27,32,32]{2,1,0:T(8,128)(2,1)}, u32[]{:S(2)}) copy-start(bf16[27,32,32]{2,1,0:T(8,128)(2,1)} %param.13) | copy-start | bytes 165892
  58.7 1.8 %copy-start.4 = (bf16[2,16,1024]{2,1,0:T(8,128)(2,1)S(1)}, bf16[2,16,1024]{2,1,0:T(8,128)(2,1)}, u32[]{:S(2)}) copy-start(bf16[2,16,1024]{2,1,0:T(8,128)(2,1)} %get-tuple-element.7) | copy-start | bytes 196612

commit v2 on v1

--- a/solution.py
+++ b/solution.py
@@ -44,8 +44,9 @@
 
 def network(
     sizes,
-    vol, hist, w1, w2, w3, w4, gf, sf, gc, sc,
+    volume, hist, c1, c2, c3, c4, gf, sf, gc, sc,
     skip_out, coarse_out, peak_out,
+    w1, w2, w3, w4, turn, vol, skip,
     stacked, prod, vals, hid, zface, yface, corner,
     pool, wide3, g3, prod3, vals3, hid3, wide4, g4,
     stat, peak, peak_all,
@@ -55,7 +56,7 @@
     zc, yc, ch, xc = vol.shape
     hz, pairs = zc // 2, yc // 4
     tiles = pairs * ny
-    oc = w3.shape[0] // 3
+    oc = c3.shape[1]
     group = ny * nz
     my_s, my_y, my_z = lax.axis_index("sample"), lax.axis_index("sy"), lax.axis_index("sz")
     me = my_y * nz + my_z
@@ -70,6 +71,17 @@
         pl.semaphore_signal(
             barrier, inc=1, device_id={"sample": lax.rem(my_s + k, ns)}, device_id_type=MESH
         )
+
+    for matrix, taps in ((w1, c1), (w2, c2), (w3, c3), (w4, c4)):
+        out = taps.shape[1]
+        for a in range(3):
+            parts = [taps[9 * a + k].astype(F32) for k in range(9)]
+            matrix[a * out : (a + 1) * out, :] = jnp.concatenate(parts, axis=1).astype(BF16)
+    for z in range(zc):
+        turn[z] = volume[:, z].astype(F32).reshape(ch * yc, LANES)
+    for z in range(zc):
+        for y in range(yc):
+            vol[z, y] = turn[z, pl.ds(y, ch, yc), :].astype(BF16)
     pl.semaphore_wait(barrier, group - 1 + ns - 1)
 
     lane = iota((ch, LANES), 1)
@@ -78,40 +90,51 @@
     def inside(dz, dy):
         z, y = my_z + dz, my_y + dy
         return (z >= 0) & (z < nz) & (y >= 0) & (y < ny)
+
+    def landing(layer, d):
+        dz, dy = STEPS[d]
+        if dy == 0:
+            return zface.at[layer, int(dz < 0)]
+        if dz == 0:
+            return yface.at[layer, int(dy < 0)]
+        return corner.at[layer, int(dz < 0) * 2 + int(dy < 0)]
 
     def halo(src, layer, d):
         dz, dy = STEPS[d]
         zi = 0 if dz < 0 else zc - 1
         yi = 0 if dy < 0 else yc - 1
         if dy == 0:
-            src, dst = src.at[zi], zface.at[layer, int(dz < 0)]
+            src = src.at[zi]
         elif dz == 0:
-            src, dst = src.at[:, yi], yface.at[layer, int(dy < 0)]
+            src = src.at[:, yi]
         else:
-            src, dst = src.at[zi, yi], corner.at[layer, int(dz < 0) * 2 + int(dy < 0)]
+            src = src.at[zi, yi]
         where = {"sy": jnp.clip(my_y + dy, 0, ny - 1), "sz": jnp.clip(my_z + dz, 0, nz - 1)}
-        return remote(src, dst, halo_s.at[layer, d], halo_r.at[layer, d], where), dst
+        return remote(src, landing(layer, d), halo_s.at[layer, d], halo_r.at[layer, d], where)
 
     def halo_start(src, layer):
         for d, (dz, dy) in enumerate(STEPS):
             @pl.when(inside(dz, dy))
             def _():
-                halo(src, layer, d)[0].start()
+                halo(src, layer, d).start()
 
             @pl.when(jnp.logical_not(inside(-dz, -dy)))
             def _():
-                dst = halo(src, layer, d)[1]
+                dst = landing(layer, d)
                 dst[...] = jnp.zeros(dst.shape, dst.dtype)
 
-    def halo_wait(src, layer):
+    def halo_wait(src, layer, flat):
         for d, (dz, dy) in enumerate(STEPS):
+            if (dz == 0) != flat:
+                continue
+
             @pl.when(inside(-dz, -dy))
             def _():
-                halo(src, layer, d)[0].wait_recv()
+                halo(src, layer, d).wait_recv()
 
             @pl.when(inside(dz, dy))
             def _():
-                halo(src, layer, d)[0].wait_send()
+                halo(src, layer, d).wait_send()
 
     def put(zp, yp, values, bound):
         v = jnp.clip(values.astype(F32), -bound, bound)
@@ -129,16 +152,19 @@
 
         return jnp.max(lax.fori_loop(0, zc, plane, jnp.zeros((ch, LANES), F32)))
 
-    def put_halo(layer, bound):
+    def put_sides(layer, bound):
+        for side in range(2):
+            for z in range(zc):
+                put(z + 1, side * (yc + 1), yface[layer, side, z], bound)
+
+    def put_ends(layer, bound):
         for side in range(2):
             for y in range(yc):
                 put(side * (zc + 1), y + 1, zface[layer, side, y], bound)
-            for z in range(zc):
-                put(z + 1, side * (yc + 1), yface[layer, side, z], bound)
             for other in range(2):
                 put(side * (zc + 1), other * (yc + 1), corner[layer, side * 2 + other], bound)
 
-    def fine_conv(w):
+    def fine_conv(w, src, layer, bound):
         def plane(zp, carry):
             for y in range(0, yc, 2):
                 rows = [stacked[zp, y + i : y + i + 3].reshape(9 * ch, LANES) for i in range(2)]
@@ -147,7 +173,12 @@
                 )
             return carry
 
-        lax.fori_loop(0, zc + 2, plane, 0)
+        halo_wait(src, layer, True)
+        put_sides(layer, bound)
+        lax.fori_loop(1, zc + 1, plane, 0)
+        halo_wait(src, layer, False)
+        put_ends(layer, bound)
+        lax.fori_loop(0, 2, lambda i, carry: plane(i * (zc + 1), carry), 0)
 
         def total(z, carry):
             s, q = carry
@@ -167,12 +198,13 @@
         return lax.fori_loop(0, zc, total, (zero, zero))
 
     def share(buf, row, index, count, send, recv, where):
-        buf[index] = jnp.broadcast_to(row, (8, LANES))
+        buf[index, 0:1, :] = row
 
         def copy(k, slot):
             other = lax.rem(index + k, count)
             at = index if slot == "mine" else other
-            return remote(buf.at[at], buf.at[at], send.at[k], recv.at[at], where(other))
+            ref = buf.at[at, pl.ds(0, 1)]
+            return remote(ref, ref, send.at[k], recv.at[at], where(other))
 
         for k in range(1, count):
             copy(k, "mine").start()
@@ -214,16 +246,12 @@
 
     halo_start(vol, 0)
     peak0 = put_inner(vol, bounds[0])
-    halo_wait(vol, 0)
-    put_halo(0, bounds[0])
-    s, q = fine_conv(w1)
+    s, q = fine_conv(w1, vol, 0, bounds[0])
     fine_act(hid, 0, s, q)
     halo_start(hid, 1)
     peak1 = put_inner(hid, bounds[1])
-    halo_wait(hid, 1)
-    put_halo(1, bounds[1])
-    s, q = fine_conv(w2)
-    fine_act(skip_out, 1, s, q)
+    s, q = fine_conv(w2, hid, 1, bounds[1])
+    fine_act(skip, 1, s, q)
 
     src_lane, dst_lane = iota((LANES, LANES), 0), iota((LANES, LANES), 1)
     half = LANES // 2
@@ -237,7 +265,7 @@
             found = jnp.zeros((ch, LANES), F32)
             for i in range(2):
                 y = 4 * t + 2 * i
-                block = [skip_out[2 * z + a, y + b].astype(F32) for a in range(2) for b in range(2)]
+                block = [skip[2 * z + a, y + b].astype(F32) for a in range(2) for b in range(2)]
                 m = jnp.maximum(jnp.maximum(block[0], block[1]), jnp.maximum(block[2], block[3]))
                 m = jnp.maximum(m, pltpu.roll(m, LANES - 1, 1))
                 found = found + jnp.dot(m.astype(BF16), pick[i], preferred_element_type=F32)
@@ -253,9 +281,9 @@
         for k in range(1, ny):
             other = lax.rem(my_y + k, ny)
             out.append((
-                None,
+                True,
                 remote(src, slab_of(my_y), send.at[0, k], recv.at[0, my_y], {"sy": other}),
-                None,
+                True,
                 remote(src, slab_of(other), send.at[0, k], recv.at[0, other], {"sy": other}),
             ))
         for kind, (step, plane, to) in enumerate(((-1, 0, hz + 1), (1, hz - 1, 0)), start=1):
@@ -273,7 +301,7 @@
         return out
 
     def guarded(flag, act):
-        if flag is None:
+        if flag is True:
             act()
         else:
             pl.when(flag)(act)
@@ -286,8 +314,10 @@
             def _():
                 buf[at] = jnp.zeros(buf.shape[1:], buf.dtype)
 
-    def coarse_wait(copies):
+    def coarse_wait(copies, slab):
         for sends, mine, gets, theirs in copies:
+            if (sends is True) != slab:
+                continue
             guarded(gets, theirs.wait_recv)
             guarded(sends, mine.wait_send)
 
@@ -296,7 +326,7 @@
         column = lax.rem(where, half)
         low = iota((3 * n, LANES), 1) < half
 
-        def plane(z, carry):
+        def plane(z):
             def put3(k, t, v):
                 wide[z, k * 3 * n : (k + 1) * 3 * n, t * LANES : (t + 1) * LANES] = v.astype(BF16)
 
@@ -313,16 +343,23 @@
                     put3(2, t - 1, jnp.where(low, before, u))
                 before = u
             put3(2, tiles - 1, jnp.where(low, before, 0.0))
-            return carry
-
-        lax.fori_loop(0, hz + 2, plane, 0)
-
-    def coarse_conv(w, wide):
+
+        return plane
+
+    def coarse_conv(w, wide, load, n, copies):
+        widen_plane = widen(load, n, wide)
+
         def plane(z, carry):
+            widen_plane(z)
             prod3[z] = jnp.dot(w[...], wide[z], preferred_element_type=F32)
             return carry
 
-        lax.fori_loop(0, hz + 2, plane, 0)
+        coarse_wait(copies, True)
+        lax.fori_loop(1, hz + 1, plane, 0)
+        coarse_wait(copies, False)
+        lax.fori_loop(0, 2, lambda i, carry: plane(i * (hz + 1), carry), 0)
+
+    def coarse_sums():
         s = q = jnp.zeros((oc, LANES), F32)
         for z in range(hz):
             for t in range(tiles):
@@ -348,9 +385,13 @@
         lambda y: g3.at[pl.ds(1, hz), pl.ds(y * pairs, pairs)],
     )
     coarse_start(copies, g3)
-    coarse_wait(copies)
-    widen(lambda z, t: g3[z, t], ch, wide3)
-    s, q = coarse_conv(w3, wide3)
+    for z in range(zc):
+        for y in range(yc):
+            turn[z, pl.ds(y, ch, yc), :] = skip[z, y].astype(F32)
+    for z in range(zc):
+        skip_out[:, z] = turn[z].reshape(ch, yc, LANES).astype(BF16)
+    coarse_conv(w3, wide3, lambda z, t: g3[z, t], ch, copies)
+    s, q = coarse_sums()
     mean, scaling, offset = moments(2, s, q, my_z, nz, slab, coarse_cells, gc[0:1, :], sc[0:1, :])
     top = jnp.zeros((oc, tiles * LANES), F32)
     for z in range(hz):
@@ -370,24 +411,26 @@
     for i, value in enumerate((peak0, peak1, peak2, peak3)):
         row = jnp.where(at == i, value, row)
     peaks = share(peak, row, me, group, pk_s, pk_r, member)
-    coarse_wait(copies)
-    widen(
-        lambda z, t: g4[z, :, :, t * LANES : (t + 1) * LANES].reshape(ny * oc, LANES), ny * oc, wide4
-    )
+
+    def cells4(z, t):
+        return g4[z, :, :, t * LANES : (t + 1) * LANES].reshape(ny * oc, LANES)
+
+    coarse_conv(w4, wide4, cells4, ny * oc, copies)
     shared(peaks, group)
     row = peak[0, 0:1, :]
     for i in range(1, group):
         row = jnp.maximum(row, peak[i, 0:1, :])
     peaks = share(peak_all, row, my_s, ns, pa_s, pa_r, lambda index: {"sample": index})
-    s, q = coarse_conv(w4, wide4)
+    s, q = coarse_sums()
     mean, scaling, offset = moments(3, s, q, my_z, nz, slab, coarse_cells, gc[1:2, :], sc[1:2, :])
     for z in range(hz):
-        coarse_out[z] = leaky((vals3[z] - mean) * scaling + offset)
+        coarse_out[:, z, :] = leaky((vals3[z] - mean) * scaling + offset)
     shared(peaks, ns)
-    row = peak_all[0]
+    row = peak_all[0, 0:1, :]
     for i in range(1, ns):
-        row = jnp.maximum(row, peak_all[i])
-    peak_out[...] = row
+        row = jnp.maximum(row, peak_all[i, 0:1, :])
+    for i in range(4):
+        peak_out[i] = jnp.max(jnp.where(at == i, row, 0.0))
 
 
 def per_device(sizes, volume, hist, c1, c2, c3, c4, gf, sf, gc, sc):
@@ -399,24 +442,26 @@
     flat = tiles * LANES
     assert xc == LANES and zc % 2 == 0 and yc % 4 == 0
 
-    def matrix(w):
-        taps, out, inner = w.shape
-        w = w.reshape(3, 9, out, inner)
-        return jnp.transpose(w, (0, 2, 1, 3)).reshape(3 * out, 9 * inner)
-
     vmem = pl.BlockSpec(memory_space=pltpu.VMEM)
     dma = pltpu.SemaphoreType.DMA
     group = ny * nz
     skip, coarse, peaks = pl.pallas_call(
         functools.partial(network, sizes),
         out_shape=(
-            jax.ShapeDtypeStruct((zc, yc, ch, xc), BF16),
-            jax.ShapeDtypeStruct((hz, oc, flat), BF16),
-            jax.ShapeDtypeStruct((8, LANES), F32),
+            jax.ShapeDtypeStruct((ch, zc, yc, xc), BF16),
+            jax.ShapeDtypeStruct((oc, hz, flat), BF16),
+            jax.ShapeDtypeStruct((4,), F32),
         ),
         in_specs=[vmem] * 10,
-        out_specs=(vmem,) * 3,
+        out_specs=(vmem, vmem, pl.BlockSpec(memory_space=pltpu.SMEM)),
         scratch_shapes=[
+            pltpu.VMEM((3 * ch, 9 * ch), BF16),
+            pltpu.VMEM((3 * ch, 9 * ch), BF16),
+            pltpu.VMEM((3 * oc, 9 * ch), BF16),
+            pltpu.VMEM((3 * oc, 9 * oc * ny), BF16),
+            pltpu.VMEM((zc, ch * yc, LANES), F32),
+            pltpu.VMEM((zc, yc, ch, LANES), BF16),
+            pltpu.VMEM((zc, yc, ch, LANES), BF16),
             pltpu.VMEM((zc + 2, yc + 2, 3 * ch, LANES), BF16),
             pltpu.VMEM((zc + 2, yc // 2, 3 * ch, 2 * LANES), F32),
             pltpu.VMEM((zc, yc, ch, LANES), F32),
@@ -449,15 +494,8 @@
         compiler_params=pltpu.CompilerParams(
             collective_id=0, has_side_effects=True, vmem_limit_bytes=56 * 1024 * 1024
         ),
-    )(
-        jnp.transpose(volume[0], (1, 2, 0, 3)),
-        hist, matrix(c1), matrix(c2), matrix(c3), matrix(c4), gf, sf, gc, sc,
-    )
-    return (
-        jnp.transpose(skip, (2, 0, 1, 3))[None],
-        jnp.transpose(coarse, (1, 0, 2))[None],
-        peaks[0, :4],
-    )
+    )(volume[0], hist, c1, c2, c3, c4, gf, sf, gc, sc)
+    return skip[None], coarse[None], peaks
 
 
 def solution(mesh):

time: 62.8 us -> 51.6 us (0.82)
  local copies, waits for them, and re-layouts: 9.61 us -> 2.85 us
  Pallas kernels: 52.1 us -> 47.9 us
    reshape x10 -> x0, local copies, waits for them, and re-layouts: 4.74 us -> none  [the longest x6 3.35 us: matrix(): return jnp.transpose(w, (0, 2, 1, 3)).reshape(3 * out, 9 * inner)]
    pallas_call x1, Pallas kernels: 52.1 us -> 47.9 us  [per_device(): pl.pallas_call(functools.partial(network, sizes), out_shape=(jax.ShapeDty...]
    squeeze x1 -> x0, local copies, waits for them, and re-layouts: 1.18 us -> none  [per_device(): peaks[0, :4]]
    unnamed x13 -> x7, local copies, waits for them, and re-layouts: 3.69 us -> 2.85 us
where the time goes in v2:
time: 51.6 us; the launch traced here: 51.4 us
  Pallas kernels  47.9 us (93%)
  local copies, waits for them, and re-layouts  2.85 us (6%)
  between operations  0.65 us (1%)
    pallas_call x1, Pallas kernels, per_device(): pl.pallas_call(functools.partial(network, sizes), out_shape=(jax.ShapeDty...  47.9 us
    unnamed x7, local copies, waits for them, and re-layouts  2.85 us

profile of v2, /device:TPU:0, one launch (start us, length us, event | category | flops | bytes accessed | tf_op | source)
XLA Modules:
  0.0 51.4 jit_solution(16708958874099726937)
XLA Ops:
  0.6 47.9 %shard_map.121 = (bf16[32,4,8,128]{3,2,1,0:T(8,128)(2,1)}, bf16[16,2,1024]{2,1,0:T(2,128)(2,1)}, f32[4]{0:T(128)}) custom-call(bf16[32,4,8,128]{3,2,1,0:T(8,128)(2,1)} %bitcast.3, f32[4,16]{1,0:T(4,128)} %hist.1, bf16[27,32,32]{2,1,0:T(8,128)(2,1)} %c1.1, bf16[27,32,32]{2,1,0:T(8,128)(2,1)} %c2.1, bf16[27,16,32]{2,1,0:T(8,128)(2,1)} %c3.1, ...), custom_call_target="tpu_custom_call" | custom-call | tf_op jit(solution)/shard_map/pallas_call | solution.py:448
  48.5 0.0 copy-start
  48.6 1.7 %copy.16 = bf16[1,32,4,8,128]{4,3,2,1,0:T(8,128)(2,1)} copy(bf16[1,32,4,8,128]{4,3,2,1,0:T(8,128)(2,1)} %bitcast.4) | data formatting | bytes 524288
  50.3 0.0 copy-done
  50.3 0.0 copy-start.1
  50.3 0.6 %copy.17 = bf16[1,16,2,1024]{3,2,1,0:T(2,128)(2,1)} copy(bf16[1,16,2,1024]{3,2,1,0:T(2,128)(2,1)S(1)} %bitcast.5) | data formatting | bytes 131072
  50.9 0.0 copy-done.1
  50.9 0.5 copy.18
Async XLA Ops:
  48.5 1.7 %copy-start = (bf16[16,2,1024]{2,1,0:T(2,128)(2,1)S(1)}, bf16[16,2,1024]{2,1,0:T(2,128)(2,1)}, u32[]{:S(2)}) copy-start(bf16[16,2,1024]{2,1,0:T(2,128)(2,1)} %get-tuple-element.7) | copy-start | bytes 196612
  50.3 0.6 %copy-start.1 = (f32[4]{0:T(128)S(1)}, f32[4]{0:T(128)}, u32[]{:S(2)}) copy-start(f32[4]{0:T(128)} %get-tuple-element.14) | copy-start | bytes 52

commit v3 on v2

--- a/solution.py
+++ b/solution.py
@@ -206,7 +206,7 @@
             ref = buf.at[at, pl.ds(0, 1)]
             return remote(ref, ref, send.at[k], recv.at[at], where(other))
 
-        for k in range(1, count):
+        for k in sorted(range(1, count), key=lambda k: -min(k % nz, -k % nz)):
             copy(k, "mine").start()
         return copy
 
@@ -495,6 +495,19 @@
             collective_id=0, has_side_effects=True, vmem_limit_bytes=56 * 1024 * 1024
         ),
     )(volume[0], hist, c1, c2, c3, c4, gf, sf, gc, sc)
+    def finish(a, b, c, oa, ob, oc_):
+        oa[...] = a[...]
+        ob[...] = b[...]
+        for i in range(4):
+            oc_[i] = c[i]
+
+    smem = pl.BlockSpec(memory_space=pltpu.SMEM)
+    skip, coarse, peaks = pl.pallas_call(
+        finish,
+        out_shape=tuple(jax.ShapeDtypeStruct(a.shape, a.dtype) for a in (skip, coarse, peaks)),
+        in_specs=[vmem, vmem, smem],
+        out_specs=(vmem, vmem, smem),
+    )(skip, coarse, peaks)
     return skip[None], coarse[None], peaks
 
 

time: 51.6 us -> 50.4 us (0.977)
  local copies, waits for them, and re-layouts: 2.85 us -> 0 us
  Pallas kernels: 47.9 us -> 49.6 us
    unnamed x7 -> x0, local copies, waits for them, and re-layouts: 2.85 us -> none
    pallas_call x0 -> x1, Pallas kernels: none -> 1.71 us  [per_device(): pl.pallas_call(finish, out_shape=tuple((jax.ShapeDtypeStruct(a.shape, a.d...]
where the time goes in v3:
time: 50.4 us; the launch traced here: 50.2 us
  Pallas kernels  49.6 us (98%)
  between operations  0.64 us (1%)
    pallas_call x1, Pallas kernels, per_device(): pl.pallas_call(functools.partial(network, sizes), out_shape=(jax.ShapeDty...  47.9 us
    pallas_call x1, Pallas kernels, per_device(): pl.pallas_call(finish, out_shape=tuple((jax.ShapeDtypeStruct(a.shape, a.d...  1.71 us

profile of v3, /device:TPU:0, one launch (start us, length us, event | category | flops | bytes accessed | tf_op | source)
XLA Modules:
  0.0 50.2 jit_solution(30258761913625799)
XLA Ops:
  0.6 47.9 %shard_map.121 = (bf16[32,4,8,128]{3,2,1,0:T(8,128)(2,1)}, bf16[16,2,1024]{2,1,0:T(2,128)(2,1)}, f32[4]{0:T(128)}) custom-call(bf16[32,4,8,128]{3,2,1,0:T(8,128)(2,1)} %bitcast.3, f32[4,16]{1,0:T(4,128)} %hist.1, bf16[27,32,32]{2,1,0:T(8,128)(2,1)} %c1.1, bf16[27,32,32]{2,1,0:T(8,128)(2,1)} %c2.1, bf16[27,16,32]{2,1,0:T(8,128)(2,1)} %c3.1, ...), custom_call_target="tpu_custom_call" | custom-call | tf_op jit(solution)/shard_map/pallas_call | solution.py:448
  48.5 1.7 %shard_map.122 = (bf16[32,4,8,128]{3,2,1,0:T(8,128)(2,1)}, bf16[16,2,1024]{2,1,0:T(2,128)(2,1)}, f32[4]{0:T(128)}) custom-call(bf16[32,4,8,128]{3,2,1,0:T(8,128)(2,1)} %get-tuple-element.9.a, bf16[16,2,1024]{2,1,0:T(2,128)(2,1)} %get-tuple-element.10.b, f32[4]{0:T(128)} %get-tuple-element.11.c), custom_call_target="tpu_custom_call" | custom-call | tf_op jit(solution)/shard_map/pallas_call | solution.py:505
